TPU v7x, 32 devices: a whole 2x2x4 slice. The times are simulated.
32 devices in a mesh: parts: 2 (over y), section: 2 (over core), tp: 8 (over z, x).
Axes of the slice: x: 2, y: 2, z: 4, core: 2. Of those that a mesh axis runs over, the one named last changes fastest.
Arguments:
- prompt_rows: bfloat16 [128, 8192], P(('parts', 'section', 'tp')), parts along dimension 0, may hold values from -72 to 72
- query_weight: bfloat16 [8192, 8192], P(None, 'tp'), may hold values from -0.0625 to 0.0625
- cache_weight: bfloat16 [8, 8192, 256], P('tp'), may hold values from -1 to 1, as said below
- output_weight: bfloat16 [8192, 8192], P('tp'), may hold values from -0.0625 to 0.0625
- documents: int32 [128], P('parts'), parts along dimension 0, may hold values from 0 to 3, never falling along the last dimension, each value on 1 to 32 neighbouring positions
- page_table: int32 [24], P('parts'), parts along dimension 0, may hold values from 0 to 15, as said below
Outputs:
- branch_output: bfloat16 [128, 8192], P(('parts', 'section', 'tp')), parts along dimension 0
- page_pool: bfloat16 [32, 8, 2048], P(('parts', 'section', 'tp')), parts along dimension 0
There are 2 independent parts, one for each index of `parts`. A program takes and returns all parts, laid end to end along the dimension named above; an argument that names none is the same for every part. Nothing has to cross between parts.
Inputs may be any that keep to these rules, and one draw needn't show every extreme that they name: `cache_weight`: entry t equals entry u whenever t == u. `documents`: ids never fall along the tokens; there are 4 prompts of 1 to 32 tokens, one of exactly 32. `page_table`: entries are distinct pool slots; slot q is owned by the device of index q along section+tp (one slot per device). Entries beyond the number of pages are not used.
All inputs are finite; a program needn't handle non-finite values.
Results may differ from a plain program's by a relative error of at most 0.0085.
The roundings to bfloat16 on the way count: a program that leaves them out, or rounds other values in their place, can miss the bound.
Values may be sent and summed in bfloat16 or wider, within the bound.
No kernel may reach another device: no remote copies, remote signals or barrier semaphores. Data moves between devices by JAX's collectives and lax.ppermute only.
A program may use at most 64 MiB of HBM per device.

v0:
```python
import jax
import jax.numpy as jnp
from jax import lax
from jax.sharding import PartitionSpec as P

KV_HEADS = 8
HEAD = 128
PAGE = 8
FEW = 8
rope_base = 500000.0


def from_partner(value, axis, mask):
    pairs = [(source, source ^ mask) for source in range(lax.axis_size(axis))]
    return lax.ppermute(value, axis, pairs)


def few_devices(count):
    return 4 <= count <= FEW and count & count - 1 == 0


def gather_rows(rows):
    count = lax.axis_size("tp")
    if not few_devices(count):
        return lax.all_gather(rows, "tp", axis=0, tiled=True)
    column = lax.axis_index("tp")
    blocks = {0: rows}
    for mask in range(2, count, 2):
        blocks[mask] = from_partner(rows, "tp", mask)
    for mask in range(0, count, 2):
        blocks[mask + 1] = from_partner(blocks[mask], "tp", 1)
    stacked = jnp.stack([blocks[mask] for mask in range(count)], axis=0)
    pieces = []
    for place in range(count):
        piece = lax.dynamic_index_in_dim(stacked, place ^ column, 0, keepdims=False)
        pieces.append(piece)
    return jnp.concatenate(pieces, axis=0)


def scatter_sum(partial, rows_dev):
    count = lax.axis_size("tp")
    if not few_devices(count):
        return lax.psum_scatter(partial, "tp", scatter_dimension=0, tiled=True)
    column = lax.axis_index("tp")
    blocks = partial.reshape(count, rows_dev, partial.shape[1])
    total = lax.dynamic_index_in_dim(blocks, column, 0, keepdims=False)
    narrow = blocks.astype(jnp.bfloat16)
    for mask in range(count - 1, 0, -1):
        sent = lax.dynamic_index_in_dim(narrow, column ^ mask, 0, keepdims=False)
        total = total + from_partner(sent, "tp", mask).astype(jnp.float32)
    return total


def document_layout(documents):
    count = documents.shape[0]
    places = jnp.arange(count, dtype=jnp.int32)
    firsts = jnp.sum((documents[None, :] < documents[:, None]).astype(jnp.int32), axis=1)
    offsets = places - firsts
    starts = (offsets % PAGE == 0)[None, :] & (places[None, :] <= places[:, None])
    pages = jnp.sum(starts.astype(jnp.int32), axis=1) - 1
    return (offsets, pages)


def rope_tables(offsets, width):
    half_width = width // 2
    freqs = rope_base ** (-(jnp.arange(half_width, dtype=jnp.float32) * 2.0 / width))
    angles = offsets.astype(jnp.float32)[:, None] * freqs[None, :]
    return (jnp.cos(angles), jnp.sin(angles))


def rotate(values, cosines, sines):
    half_width = values.shape[-1] // 2
    first = values[..., :half_width]
    second = values[..., half_width:]
    return jnp.concatenate(
        [first * cosines - second * sines, second * cosines + first * sines], axis=-1
    )


def finish_cache(keyvals, cosines, sines):
    rotated = rotate(keyvals[:, :HEAD], cosines, sines)
    return jnp.concatenate([rotated, keyvals[:, HEAD:]], axis=1).astype(jnp.bfloat16)


def body(prompt_rows, query_weight, cache_weight, output_weight, documents, page_table):
    tp_count = lax.axis_size("tp")
    owners = lax.axis_size(("section", "tp"))
    section = lax.axis_index("section")
    column = lax.axis_index("tp")
    rows_dev = prompt_rows.shape[0]
    half_rows = rows_dev * tp_count
    total_rows = 2 * half_rows
    query_width = query_weight.shape[1]
    query_heads = query_width // HEAD
    replicas = tp_count // KV_HEADS
    slice_width = HEAD // replicas
    head_weight = cache_weight[0]
    offsets, pages = document_layout(documents)
    cosines, sines = rope_tables(offsets, HEAD)
    own_start = section * half_rows
    own_cos = lax.dynamic_slice_in_dim(cosines, own_start, half_rows, 0)
    own_sin = lax.dynamic_slice_in_dim(sines, own_start, half_rows, 0)
    piece = gather_rows(prompt_rows)
    cache_rows = jnp.dot(piece, head_weight, preferred_element_type=jnp.float32)
    query_part = jnp.dot(piece, query_weight, preferred_element_type=jnp.float32)
    cache_half = finish_cache(cache_rows, own_cos, own_sin)
    other = from_partner(cache_half, "section", 1)
    lower = jnp.where(section == 0, cache_half, other)
    upper = jnp.where(section == 0, other, cache_half)
    cache_all = jnp.concatenate([lower, upper], axis=0)
    queries = query_part.reshape(half_rows, query_heads, HEAD)
    queries = rotate(queries, own_cos[:, None, :], own_sin[:, None, :]).astype(jnp.bfloat16)
    keys = cache_all[:, :HEAD]
    values = cache_all[:, HEAD:]
    places = jnp.arange(total_rows, dtype=jnp.int32)
    query_places = own_start + jnp.arange(half_rows, dtype=jnp.int32)
    query_docs = lax.dynamic_slice_in_dim(documents, own_start, half_rows, 0)
    allowed = (query_docs[:, None] == documents[None, :]) & (
        places[None, :] <= query_places[:, None]
    )
    scale = 1.0 / HEAD**0.5
    scores = jnp.einsum("qhd,kd->hqk", queries, keys, preferred_element_type=jnp.float32) * scale
    scores = jnp.where(allowed[None, :, :], scores, -jnp.inf)
    weights = jax.nn.softmax(scores, axis=-1).astype(jnp.bfloat16)
    mixed = jnp.einsum("hqk,kd->qhd", weights, values, preferred_element_type=jnp.float32)
    attention = mixed.astype(jnp.bfloat16).reshape(half_rows, query_heads * HEAD)
    column_start = section * HEAD + column % replicas * slice_width
    share = lax.dynamic_slice_in_dim(cache_all, column_start, slice_width, 1)
    capacity = rows_dev // 4 * PAGE
    slots = jnp.arange(page_table.shape[0], dtype=jnp.int32)
    hit = pages[:, None] == slots[None, :]
    table_at = jnp.sum(jnp.where(hit, page_table[None, :], 0), axis=1)
    row_of = table_at * PAGE + offsets % PAGE
    pool_rows = jnp.arange(owners * capacity, dtype=jnp.int32)
    placed = (pool_rows[:, None] == row_of[None, :]).astype(jnp.bfloat16)
    outgoing = jnp.dot(placed, share, preferred_element_type=jnp.float32).astype(jnp.bfloat16)
    outgoing = outgoing.reshape(owners, capacity, slice_width)
    arrived = lax.all_to_all(outgoing, ("section", "tp"), split_axis=0, concat_axis=2, tiled=True)
    partial = jnp.dot(attention, output_weight, preferred_element_type=jnp.float32)
    branch_output = scatter_sum(partial, rows_dev).astype(jnp.bfloat16)
    return (branch_output, arrived)


def solution(mesh):
    return jax.shard_map(
        body,
        mesh=mesh,
        in_specs=(
            P(("parts", "section", "tp"), None),
            P(None, "tp"),
            P("tp", None, None),
            P("tp", None),
            P("parts"),
            P("parts"),
        ),
        out_specs=(P(("parts", "section", "tp"), None), P(("parts", "section", "tp"), None, None)),
        check_vma=False,
    )
```

profile of v0, /device:TPU:0, one launch (start us, length us, event | category | flops | bytes accessed | tf_op | source)
XLA Modules:
  0.0 67.6 jit_solution(11010513600274081855)
XLA Ops:
  0.6 3.1 %collective-permute-start.1 = (bf16[4,8192]{1,0:T(4,128)(2,1)}, bf16[4,8192]{1,0:T(4,128)(2,1)S(1)}, u32[]{:S(2)}, u32[]{:S(2)}) collective-permute-start(bf16[4,8192]{1,0:T(4,128)(2,1)} %param.6), channel_id=1, source_target_pairs={{0,2},{1,3},{2,0},{3,1},{4,6},{5,7},{6,4},{7,5},{8,10},{9,11},{10,... | collective-permute-start | bytes 196616 | tf_op jit(solution)/shard_map/ppermute | solution.py:15
  3.7 1.5 %collective-permute-start = (bf16[4,8192]{1,0:T(4,128)(2,1)}, bf16[4,8192]{1,0:T(4,128)(2,1)S(1)}, u32[]{:S(2)}, u32[]{:S(2)}) collective-permute-start(bf16[4,8192]{1,0:T(4,128)(2,1)} %param.6), channel_id=1, source_target_pairs={{0,1},{1,0},{2,3},{3,2},{4,5},{5,4},{6,7},{7,6},{8,9},{9,8},{10,11... | collective-permute-start | bytes 196616 | tf_op jit(solution)/shard_map/ppermute | solution.py:15
  5.2 2.5 %collective-permute-start.5 = (bf16[4,8192]{1,0:T(4,128)(2,1)}, bf16[4,8192]{1,0:T(4,128)(2,1)S(1)}, u32[]{:S(2)}, u32[]{:S(2)}) collective-permute-start(bf16[4,8192]{1,0:T(4,128)(2,1)} %param.6), channel_id=1, source_target_pairs={{0,6},{1,7},{2,4},{3,5},{4,2},{5,3},{6,0},{7,1},{8,14},{9,15},{10,... | collective-permute-start | bytes 196616 | tf_op jit(solution)/shard_map/ppermute | solution.py:15
  7.7 0.1 collective-permute-start.3
  7.8 0.9 %convert_reduce_fusion.1 = s32[64]{0:T(128)S(1)} fusion(s32[64]{0:T(128)} %param.10), kind=kLoop, calls=%fused_computation.63 | loop fusion | flops 12224 | bytes 512 | tf_op jit(solution)/shard_map/reduce_sum | solution.py:57
  8.8 0.9 %bitcast_dynamic-update-slice_fusion.7 = bf16[8,4,8192]{2,1,0:T(4,128)(2,1)S(1)} fusion(bf16[4,8192]{1,0:T(4,128)(2,1)} %param.6), kind=kLoop, calls=%fused_computation.43 | loop fusion | bytes 131072
  9.7 0.7 %dynamic_slice.72 = s32[32]{0:T(128)S(1)} dynamic-slice(s32[64]{0:T(128)} %param.10, s32[]{:T(128)S(6)} %select_n.91), dynamic_slice_sizes={32} | dynamic-slice | bytes 260 | tf_op jit(solution)/shard_map/dynamic_slice | solution.py:117
  10.4 0.1 convert_reduce_fusion
  10.5 0.7 %select_reduce_fusion = s32[64]{0:T(128)S(1)} fusion(s32[12]{0:T(128)} %param.11, s32[64]{0:T(128)S(1)} %broadcast_add_fusion), kind=kLoop, calls=%fused_computation.81 | loop fusion | flops 2240 | bytes 560 | tf_op jit(solution)/shard_map/reduce_sum | solution.py:132
  11.3 0.7 %fusion.32 = pred[32,64]{1,0:T(8,128)(4,1)S(1)} fusion(s32[32]{0:T(128)S(1)} %iota_add_fusion, s32[64]{0:T(128)} %param.10, s32[32]{0:T(128)S(1)} %dynamic_slice.72), kind=kLoop, calls=%fused_computation.76 | loop fusion | flops 6144 | bytes 2560 | tf_op jit(solution)/shard_map/and | solution.py:118
  12.0 0.1 broadcast_multiply_fusion
  12.1 0.0 collective-permute-done.1
  12.1 0.6 collective-permute-start.2
  12.7 0.0 collective-permute-done.5
  12.7 1.5 %collective-permute-start.6 = (bf16[4,8192]{1,0:T(4,128)(2,1)S(1)}, bf16[4,8192]{1,0:T(4,128)(2,1)S(1)}, u32[]{:S(2)}, u32[]{:S(2)}) collective-permute-start(bf16[4,8192]{1,0:T(4,128)(2,1)S(1)} %collective-permute-done.5), channel_id=1, source_target_pairs={{0,1},{1,0},{2,3},{3,2},{4,5},{5,4},{6,7},{7,6},{8,9},{9,8},{10,11... | collective-permute-start | bytes 196616 | tf_op jit(solution)/shard_map/ppermute | solution.py:15
  14.2 0.0 collective-permute-done.3
  14.2 0.6 collective-permute-start.4
  14.8 0.0 collective-permute-done
  14.9 1.7 %collective-permute-done.2 = bf16[4,8192]{1,0:T(4,128)(2,1)S(1)} collective-permute-done((bf16[4,8192]{1,0:T(4,128)(2,1)S(1)}, bf16[4,8192]{1,0:T(4,128)(2,1)S(1)}, u32[]{:S(2)}, u32[]{:S(2)}) %collective-permute-start.2) | collective-permute-done | bytes 65568 | tf_op jit(solution)/shard_map/ppermute | solution.py:15
  16.7 1.9 %collective-permute-done.4 = bf16[4,8192]{1,0:T(4,128)(2,1)S(1)} collective-permute-done((bf16[4,8192]{1,0:T(4,128)(2,1)S(1)}, bf16[4,8192]{1,0:T(4,128)(2,1)S(1)}, u32[]{:S(2)}, u32[]{:S(2)}) %collective-permute-start.4) | collective-permute-done | bytes 65568 | tf_op jit(solution)/shard_map/ppermute | solution.py:15
  18.6 0.0 collective-permute-done.6
  18.7 0.2 dynamic-slice_bitcast_fusion
  18.9 0.3 concatenate.14
  19.3 3.0 %fusion.3 = f32[32,256]{1,0:T(8,128)S(1)} fusion(bf16[32,8192]{1,0:T(8,128)(2,1)S(1)} %concatenate.14, bf16[1,8192,256]{2,1,0:T(8,128)(2,1)} %param.8), kind=kOutput, calls=%fused_computation.3 | convolution fusion | flops 134217728 | bytes 4751360 | tf_op jit(solution)/shard_map/dot_general | solution.py:104
  22.3 8.8 %convolution_bitcast_fusion = f32[4,8,8,128]{3,1,2,0:T(8,128)S(1)} fusion(bf16[32,8192]{1,0:T(8,128)(2,1)S(1)} %concatenate.14, bf16[8192,1024]{1,0:T(8,128)(2,1)} %param.7), kind=kOutput, calls=%fused_computation.7 | convolution fusion | flops 536870912 | bytes 17432576 | tf_op jit(solution)/shard_map/dot_general | solution.py:105
  31.1 0.1 subtract_convert_fusion.1
  31.2 0.1 add_convert_fusion.1
  31.2 0.1 pad_maximum_fusion
  31.3 0.0 collective-permute-start.7
  31.3 0.1 fusion.66
  31.4 0.1 subtract_convert_fusion
  31.5 1.0 %collective-permute-done.7 = bf16[32,256]{1,0:T(8,128)(2,1)S(1)} collective-permute-done((bf16[32,256]{1,0:T(8,128)(2,1)S(1)}, bf16[32,256]{1,0:T(8,128)(2,1)S(1)}, u32[]{:S(2)}, u32[]{:S(2)}) %collective-permute-start.7) | collective-permute-done | bytes 16416 | tf_op jit(solution)/shard_map/ppermute | solution.py:15
  32.5 0.1 broadcast_select_fusion
  32.6 0.4 fusion.67
  33.0 0.6 fusion.9
  33.6 8.6 %fusion.72 = (bf16[8,4,8192]{2,0,1:T(8,128)(2,1)S(1)}, f32[8,4,8192]{2,0,1:T(8,128)S(1)}) fusion(bf16[1024,8192]{1,0:T(8,128)(2,1)} %param.9, bf16[8,4,1024]{2,1,0:T(4,128)(2,1)S(1)} %dot_general.24), kind=kOutput, calls=%fused_computation.114 | convolution fusion | flops 537133056 | bytes 18415616 | tf_op jit(solution)/shard_map/dot_general | solution.py:139
  42.3 1.0 %constant_dynamic-slice_fusion.6 = (bf16[1,4,8192]{2,0,1:T(2,128)(2,1)S(1)}, bf16[1,4,8192]{2,0,1:T(2,128)(2,1)S(1)}, bf16[1,4,8192]{2,0,1:T(2,128)(2,1)S(1)}, b...) fusion(bf16[8,4,8192]{2,0,1:T(8,128)(2,1)S(1)} %get-tuple-eleme, ...), kind=kLoop, calls=%fused_computation.89 | loop fusion | bytes 917532 | tf_op jit(solution)/shard_map/jit(dynamic_index_in_dim)/dynamic_slice | solution.py:49
  43.3 0.1 copy.51
  43.4 0.1 copy.52
  43.5 2.9 %collective-permute-start.9 = (bf16[4,8192]{1,0:T(4,128)(2,1)S(1)}, bf16[4,8192]{1,0:T(4,128)(2,1)S(1)}, u32[]{:S(2)}, u32[]{:S(2)}) collective-permute-start(bf16[4,8192]{1,0:T(4,128)(2,1)S(1)} %bitcast.129), channel_id=1, source_target_pairs={{0,6},{1,7},{2,4},{3,5},{4,2},{5,3},{6,0},{7,1},{8,14},{9,15},{10,... | collective-permute-start | bytes 196616 | tf_op jit(solution)/shard_map/ppermute | solution.py:15
  46.4 0.5 collective-permute-start.10
  46.9 0.7 %fusion.10 = bf16[16,8,128]{2,1,0:T(8,128)(2,1)} fusion(s32[64]{0:T(128)S(1)} %multiply_add_fusion, s32[]{:T(128)S(6)} %select_n.97, bf16[32,256]{1,0:T(8,128)(2,1)S(1)} %get-tuple-element.27, bf16[32,256]{1,0:T(8,128)(2,1)S(1)} %get-tuple-element.26), kind=kOutput, calls=%fused_computation.14 | convolution fusion | flops 2154496 | bytes 65796 | tf_op jit(solution)/shard_map/dot_general | solution.py:136
  47.6 4.7 %all-to-all-start = ((bf16[16,8,128]{2,1,0:T(8,128)(2,1)}), bf16[16,8,128]{2,1,0:T(8,128)(2,1)S(1)}, u32[]{:S(2)}, u32[]{:S(2)}) async-start(bf16[16,8,128]{2,1,0:T(8,128)(2,1)} %fusion.10), calls=%async_computation | async-start | bytes 65536 | tf_op jit(solution)/shard_map/all_to_all | solution.py:138
  52.4 0.1 copy.53
  52.5 0.1 copy.47
  52.6 0.1 copy.48
  52.7 0.1 copy.49
  52.8 0.1 copy.50
  52.9 2.9 %collective-permute-start.11 = (bf16[4,8192]{1,0:T(4,128)(2,1)S(1)}, bf16[4,8192]{1,0:T(4,128)(2,1)S(1)}, u32[]{:S(2)}, u32[]{:S(2)}) collective-permute-start(bf16[4,8192]{1,0:T(4,128)(2,1)S(1)} %bitcast.130), channel_id=1, source_target_pairs={{0,4},{1,5},{2,6},{3,7},{4,0},{5,1},{6,2},{7,3},{8,12},{9,13},{10,... | collective-permute-start | bytes 196616 | tf_op jit(solution)/shard_map/ppermute | solution.py:15
  55.7 2.4 %collective-permute-start.12 = (bf16[4,8192]{1,0:T(4,128)(2,1)S(1)}, bf16[4,8192]{1,0:T(4,128)(2,1)S(1)}, u32[]{:S(2)}, u32[]{:S(2)}) collective-permute-start(bf16[4,8192]{1,0:T(4,128)(2,1)S(1)} %bitcast.128), channel_id=1, source_target_pairs={{0,3},{1,2},{2,1},{3,0},{4,7},{5,6},{6,5},{7,4},{8,11},{9,10},{10,... | collective-permute-start | bytes 196616 | tf_op jit(solution)/shard_map/ppermute | solution.py:15
  58.1 0.6 collective-permute-start.13
  58.7 0.0 collective-permute-done.9
  58.7 0.6 collective-permute-start.14
  59.2 0.0 collective-permute-done.10
  59.2 2.4 %collective-permute-start.8 = (bf16[4,8192]{1,0:T(4,128)(2,1)S(1)}, bf16[4,8192]{1,0:T(4,128)(2,1)S(1)}, u32[]{:S(2)}, u32[]{:S(2)}) collective-permute-start(bf16[4,8192]{1,0:T(4,128)(2,1)S(1)} %bitcast.124), channel_id=1, source_target_pairs={{0,7},{1,6},{2,5},{3,4},{4,3},{5,2},{6,1},{7,0},{8,15},{9,14},{10,... | collective-permute-start | bytes 196616 | tf_op jit(solution)/shard_map/ppermute | solution.py:15
  61.6 0.1 constant_dynamic-slice_fusion.7
  61.7 0.0 all-to-all-done
  61.7 0.0 collective-permute-done.11
  61.7 0.4 collective-permute-done.12
  62.1 0.4 collective-permute-done.13
  62.5 0.4 collective-permute-done.14
  62.9 3.3 %collective-permute-done.8 = bf16[4,8192]{1,0:T(4,128)(2,1)S(1)} collective-permute-done((bf16[4,8192]{1,0:T(4,128)(2,1)S(1)}, bf16[4,8192]{1,0:T(4,128)(2,1)S(1)}, u32[]{:S(2)}, u32[]{:S(2)}) %collective-permute-start.8) | collective-permute-done | bytes 65568 | tf_op jit(solution)/shard_map/ppermute | solution.py:15
  66.2 0.8 %fusion.17 = bf16[4,8192]{1,0:T(4,128)(2,1)} fusion(bf16[4,8192]{1,0:T(4,128)(2,1)S(1)} %collective-permute-done.14, bf16[4,8192]{1,0:T(4,128)(2,1)S(1)} %collective-permute-done.13, bf16[4,8192]{1,0:T(4,128)(2,1)S(1)} %collective-permute-done.12, bf16[4,8192]{1,0:T(4,128)(2,1)S(1)} %collective-permute-done.11, ...), kind=kLoop, calls=%fused_computation.25 | loop fusion | flops 491520 | bytes 655360 | tf_op jit(solution)/shard_map/convert_element_type | solution.py:140
  67.0 0.6 copy.62
  (17 shorter events, 0.4 us)
Async XLA Ops:
  0.6 11.5 %collective-permute-start.1 = (bf16[4,8192]{1,0:T(4,128)(2,1)}, bf16[4,8192]{1,0:T(4,128)(2,1)S(1)}, u32[]{:S(2)}, u32[]{:S(2)}) collective-permute-start(bf16[4,8192]{1,0:T(4,128)(2,1)} %param.6), channel_id=1, source_target_pairs={{0,2},{1,3},{2,0},{3,1},{4,6},{5,7},{6,4},{7,5},{8,10},{9,11},{10,... | collective-permute-start | bytes 196616 | tf_op jit(solution)/shard_map/ppermute | solution.py:15
  3.7 11.1 %collective-permute-start = (bf16[4,8192]{1,0:T(4,128)(2,1)}, bf16[4,8192]{1,0:T(4,128)(2,1)S(1)}, u32[]{:S(2)}, u32[]{:S(2)}) collective-permute-start(bf16[4,8192]{1,0:T(4,128)(2,1)} %param.6), channel_id=1, source_target_pairs={{0,1},{1,0},{2,3},{3,2},{4,5},{5,4},{6,7},{7,6},{8,9},{9,8},{10,11... | collective-permute-start | bytes 196616 | tf_op jit(solution)/shard_map/ppermute | solution.py:15
  5.2 7.5 %collective-permute-start.5 = (bf16[4,8192]{1,0:T(4,128)(2,1)}, bf16[4,8192]{1,0:T(4,128)(2,1)S(1)}, u32[]{:S(2)}, u32[]{:S(2)}) collective-permute-start(bf16[4,8192]{1,0:T(4,128)(2,1)} %param.6), channel_id=1, source_target_pairs={{0,6},{1,7},{2,4},{3,5},{4,2},{5,3},{6,0},{7,1},{8,14},{9,15},{10,... | collective-permute-start | bytes 196616 | tf_op jit(solution)/shard_map/ppermute | solution.py:15
  7.7 6.5 %collective-permute-start.3 = (bf16[4,8192]{1,0:T(4,128)(2,1)}, bf16[4,8192]{1,0:T(4,128)(2,1)S(1)}, u32[]{:S(2)}, u32[]{:S(2)}) collective-permute-start(bf16[4,8192]{1,0:T(4,128)(2,1)} %param.6), channel_id=1, source_target_pairs={{0,4},{1,5},{2,6},{3,7},{4,0},{5,1},{6,2},{7,3},{8,12},{9,13},{10,... | collective-permute-start | bytes 196616 | tf_op jit(solution)/shard_map/ppermute | solution.py:15
  12.1 4.5 %collective-permute-start.2 = (bf16[4,8192]{1,0:T(4,128)(2,1)S(1)}, bf16[4,8192]{1,0:T(4,128)(2,1)S(1)}, u32[]{:S(2)}, u32[]{:S(2)}) collective-permute-start(bf16[4,8192]{1,0:T(4,128)(2,1)S(1)} %collective-permute-done.1), channel_id=1, source_target_pairs={{0,1},{1,0},{2,3},{3,2},{4,5},{5,4},{6,7},{7,6},{8,9},{9,8},{10,11... | collective-permute-start | bytes 196616 | tf_op jit(solution)/shard_map/ppermute | solution.py:15
  12.7 5.9 %collective-permute-start.6 = (bf16[4,8192]{1,0:T(4,128)(2,1)S(1)}, bf16[4,8192]{1,0:T(4,128)(2,1)S(1)}, u32[]{:S(2)}, u32[]{:S(2)}) collective-permute-start(bf16[4,8192]{1,0:T(4,128)(2,1)S(1)} %collective-permute-done.5), channel_id=1, source_target_pairs={{0,1},{1,0},{2,3},{3,2},{4,5},{5,4},{6,7},{7,6},{8,9},{9,8},{10,11... | collective-permute-start | bytes 196616 | tf_op jit(solution)/shard_map/ppermute | solution.py:15
  14.2 4.3 %collective-permute-start.4 = (bf16[4,8192]{1,0:T(4,128)(2,1)S(1)}, bf16[4,8192]{1,0:T(4,128)(2,1)S(1)}, u32[]{:S(2)}, u32[]{:S(2)}) collective-permute-start(bf16[4,8192]{1,0:T(4,128)(2,1)S(1)} %collective-permute-done.3), channel_id=1, source_target_pairs={{0,1},{1,0},{2,3},{3,2},{4,5},{5,4},{6,7},{7,6},{8,9},{9,8},{10,11... | collective-permute-start | bytes 196616 | tf_op jit(solution)/shard_map/ppermute | solution.py:15
  31.3 1.2 %collective-permute-start.7 = (bf16[32,256]{1,0:T(8,128)(2,1)S(1)}, bf16[32,256]{1,0:T(8,128)(2,1)S(1)}, u32[]{:S(2)}, u32[]{:S(2)}) collective-permute-start(bf16[32,256]{1,0:T(8,128)(2,1)S(1)} %pad_maximum_fusion), channel_id=1, source_target_pairs={{0,8},{8,0},{1,9},{9,1},{2,10},{10,2},{3,11},{11,3},{4,12},{12,4},... | collective-permute-start | bytes 49160 | tf_op jit(solution)/shard_map/ppermute | solution.py:15
  43.5 15.2 %collective-permute-start.9 = (bf16[4,8192]{1,0:T(4,128)(2,1)S(1)}, bf16[4,8192]{1,0:T(4,128)(2,1)S(1)}, u32[]{:S(2)}, u32[]{:S(2)}) collective-permute-start(bf16[4,8192]{1,0:T(4,128)(2,1)S(1)} %bitcast.129), channel_id=1, source_target_pairs={{0,6},{1,7},{2,4},{3,5},{4,2},{5,3},{6,0},{7,1},{8,14},{9,15},{10,... | collective-permute-start | bytes 196616 | tf_op jit(solution)/shard_map/ppermute | solution.py:15
  46.4 12.8 %collective-permute-start.10 = (bf16[4,8192]{1,0:T(4,128)(2,1)S(1)}, bf16[4,8192]{1,0:T(4,128)(2,1)S(1)}, u32[]{:S(2)}, u32[]{:S(2)}) collective-permute-start(bf16[4,8192]{1,0:T(4,128)(2,1)S(1)} %bitcast.126), channel_id=1, source_target_pairs={{0,5},{1,4},{2,7},{3,6},{4,1},{5,0},{6,3},{7,2},{8,13},{9,12},{10,... | collective-permute-start | bytes 196616 | tf_op jit(solution)/shard_map/ppermute | solution.py:15
  47.6 14.1 %all-to-all-start = ((bf16[16,8,128]{2,1,0:T(8,128)(2,1)}), bf16[16,8,128]{2,1,0:T(8,128)(2,1)S(1)}, u32[]{:S(2)}, u32[]{:S(2)}) async-start(bf16[16,8,128]{2,1,0:T(8,128)(2,1)} %fusion.10), calls=%async_computation | async-start | bytes 65536 | tf_op jit(solution)/shard_map/all_to_all | solution.py:138
  52.9 8.9 %collective-permute-start.11 = (bf16[4,8192]{1,0:T(4,128)(2,1)S(1)}, bf16[4,8192]{1,0:T(4,128)(2,1)S(1)}, u32[]{:S(2)}, u32[]{:S(2)}) collective-permute-start(bf16[4,8192]{1,0:T(4,128)(2,1)S(1)} %bitcast.130), channel_id=1, source_target_pairs={{0,4},{1,5},{2,6},{3,7},{4,0},{5,1},{6,2},{7,3},{8,12},{9,13},{10,... | collective-permute-start | bytes 196616 | tf_op jit(solution)/shard_map/ppermute | solution.py:15
  55.7 6.4 %collective-permute-start.12 = (bf16[4,8192]{1,0:T(4,128)(2,1)S(1)}, bf16[4,8192]{1,0:T(4,128)(2,1)S(1)}, u32[]{:S(2)}, u32[]{:S(2)}) collective-permute-start(bf16[4,8192]{1,0:T(4,128)(2,1)S(1)} %bitcast.128), channel_id=1, source_target_pairs={{0,3},{1,2},{2,1},{3,0},{4,7},{5,6},{6,5},{7,4},{8,11},{9,10},{10,... | collective-permute-start | bytes 196616 | tf_op jit(solution)/shard_map/ppermute | solution.py:15
  58.1 4.4 %collective-permute-start.13 = (bf16[4,8192]{1,0:T(4,128)(2,1)S(1)}, bf16[4,8192]{1,0:T(4,128)(2,1)S(1)}, u32[]{:S(2)}, u32[]{:S(2)}) collective-permute-start(bf16[4,8192]{1,0:T(4,128)(2,1)S(1)} %bitcast.127), channel_id=1, source_target_pairs={{0,2},{1,3},{2,0},{3,1},{4,6},{5,7},{6,4},{7,5},{8,10},{9,11},{10,... | collective-permute-start | bytes 196616 | tf_op jit(solution)/shard_map/ppermute | solution.py:15
  58.7 4.3 %collective-permute-start.14 = (bf16[4,8192]{1,0:T(4,128)(2,1)S(1)}, bf16[4,8192]{1,0:T(4,128)(2,1)S(1)}, u32[]{:S(2)}, u32[]{:S(2)}) collective-permute-start(bf16[4,8192]{1,0:T(4,128)(2,1)S(1)} %bitcast.125), channel_id=1, source_target_pairs={{0,1},{1,0},{2,3},{3,2},{4,5},{5,4},{6,7},{7,6},{8,9},{9,8},{10,11... | collective-permute-start | bytes 196616 | tf_op jit(solution)/shard_map/ppermute | solution.py:15
  59.2 7.0 %collective-permute-start.8 = (bf16[4,8192]{1,0:T(4,128)(2,1)S(1)}, bf16[4,8192]{1,0:T(4,128)(2,1)S(1)}, u32[]{:S(2)}, u32[]{:S(2)}) collective-permute-start(bf16[4,8192]{1,0:T(4,128)(2,1)S(1)} %bitcast.124), channel_id=1, source_target_pairs={{0,7},{1,6},{2,5},{3,4},{4,3},{5,2},{6,1},{7,0},{8,15},{9,14},{10,... | collective-permute-start | bytes 196616 | tf_op jit(solution)/shard_map/ppermute | solution.py:15
where the time goes:
time: 68 us; the launch traced here: 67.6 us
  starting transfers between devices  26.7 us (39%)
  matrix products  22.1 us (32%)
  waiting for transfers between devices  9.11 us (13%)
  local copies, waits for them, and re-layouts  4.95 us (7%)
  other arithmetic  3.81 us (6%)
  between operations  0.92 us (1%)
    ppermute x15, starting transfers between devices, from_partner(): return lax.ppermute(value, axis, pairs)  22 us
    ppermute x15, waiting for transfers between devices, from_partner(): return lax.ppermute(value, axis, pairs)  9.11 us
    dot_general x1, matrix products, body(): jnp.dot(piece, query_weight, preferred_element_type=jnp.float32)  8.76 us
    dot_general x1, matrix products, body(): jnp.dot(attention, output_weight, preferred_element_type=jnp.float32)  8.63 us
    all_to_all x1, starting transfers between devices, body(): lax.all_to_all(outgoing, ('section', 'tp'), split_axis=0, concat_axis=2,...  4.73 us
    dot_general x1, matrix products, body(): cache_rows = jnp.dot(piece, head_weight, preferred_element_type=jnp.float32)  3.01 us
    unnamed x16, local copies, waits for them, and re-layouts  2.34 us
  transfers between devices with their start and end apart: 16, of which 7 were waited for; matrix products, arithmetic and copies ran while one was open for 9% of the time, Pallas kernels for 0%

commit v1 on v0

--- a/solution.py
+++ b/solution.py
@@ -135,7 +135,9 @@
     placed = (pool_rows[:, None] == row_of[None, :]).astype(jnp.bfloat16)
     outgoing = jnp.dot(placed, share, preferred_element_type=jnp.float32).astype(jnp.bfloat16)
     outgoing = outgoing.reshape(owners, capacity, slice_width)
-    arrived = lax.all_to_all(outgoing, ("section", "tp"), split_axis=0, concat_axis=2, tiled=True)
+    parts = jnp.split(outgoing, lax.axis_size(("section", "tp")), axis=0)
+    received = lax.all_to_all(jnp.stack(parts), ("section", "tp"), 0, 0)
+    arrived = jnp.concatenate(received, axis=2)
     partial = jnp.dot(attention, output_weight, preferred_element_type=jnp.float32)
     branch_output = scatter_sum(partial, rows_dev).astype(jnp.bfloat16)
     return (branch_output, arrived)

time: 68 us -> 76.7 us (1.13)
  local copies, waits for them, and re-layouts: 4.95 us -> 14.2 us
    unnamed x16 -> x31, local copies, waits for them, and re-layouts: 2.34 us -> 11 us
  transfers between devices with their start and end apart: 16 -> 16, of which waited for: 7 -> 7; matrix products, arithmetic and copies ran while one was open for 9% -> 7% of each run, Pallas kernels for 0% -> 0%
where the time goes in v1:
time: 76.7 us; the launch traced here: 76.3 us
  starting transfers between devices  26.7 us (35%)
  matrix products  21.5 us (28%)
  local copies, waits for them, and re-layouts  14.2 us (19%)
  waiting for transfers between devices  9.11 us (12%)
  other arithmetic  3.81 us (5%)
  between operations  0.92 us (1%)
    ppermute x15, starting transfers between devices, from_partner(): return lax.ppermute(value, axis, pairs)  22 us
    unnamed x31, local copies, waits for them, and re-layouts  11 us
    ppermute x15, waiting for transfers between devices, from_partner(): return lax.ppermute(value, axis, pairs)  9.11 us
    dot_general x1, matrix products, body(): jnp.dot(piece, query_weight, preferred_element_type=jnp.float32)  8.76 us
    dot_general x1, matrix products, body(): jnp.dot(attention, output_weight, preferred_element_type=jnp.float32)  8.62 us
    all_to_all x1, starting transfers between devices, body(): received = lax.all_to_all(jnp.stack(parts), ('section', 'tp'), 0, 0)  4.73 us
    dot_general x1, matrix products, body(): cache_rows = jnp.dot(piece, head_weight, preferred_element_type=jnp.float32)  3.01 us
  transfers between devices with their start and end apart: 16, of which 7 were waited for; matrix products, arithmetic and copies ran while one was open for 7% of the time, Pallas kernels for 0%

profile of v1, /device:TPU:0, one launch (start us, length us, event | category | flops | bytes accessed | tf_op | source)
XLA Modules:
  0.0 76.3 jit_solution(11264101624380478542)
XLA Ops:
  0.6 3.1 %collective-permute-start.1 = (bf16[4,8192]{1,0:T(4,128)(2,1)}, bf16[4,8192]{1,0:T(4,128)(2,1)S(1)}, u32[]{:S(2)}, u32[]{:S(2)}) collective-permute-start(bf16[4,8192]{1,0:T(4,128)(2,1)} %param.6), channel_id=1, source_target_pairs={{0,2},{1,3},{2,0},{3,1},{4,6},{5,7},{6,4},{7,5},{8,10},{9,11},{10,... | collective-permute-start | bytes 196616 | tf_op jit(solution)/shard_map/ppermute | solution.py:15
  3.7 1.5 %collective-permute-start = (bf16[4,8192]{1,0:T(4,128)(2,1)}, bf16[4,8192]{1,0:T(4,128)(2,1)S(1)}, u32[]{:S(2)}, u32[]{:S(2)}) collective-permute-start(bf16[4,8192]{1,0:T(4,128)(2,1)} %param.6), channel_id=1, source_target_pairs={{0,1},{1,0},{2,3},{3,2},{4,5},{5,4},{6,7},{7,6},{8,9},{9,8},{10,11... | collective-permute-start | bytes 196616 | tf_op jit(solution)/shard_map/ppermute | solution.py:15
  5.2 2.5 %collective-permute-start.5 = (bf16[4,8192]{1,0:T(4,128)(2,1)}, bf16[4,8192]{1,0:T(4,128)(2,1)S(1)}, u32[]{:S(2)}, u32[]{:S(2)}) collective-permute-start(bf16[4,8192]{1,0:T(4,128)(2,1)} %param.6), channel_id=1, source_target_pairs={{0,6},{1,7},{2,4},{3,5},{4,2},{5,3},{6,0},{7,1},{8,14},{9,15},{10,... | collective-permute-start | bytes 196616 | tf_op jit(solution)/shard_map/ppermute | solution.py:15
  7.7 0.1 collective-permute-start.3
  7.8 0.9 %convert_reduce_fusion.1 = s32[64]{0:T(128)S(1)} fusion(s32[64]{0:T(128)} %param.10), kind=kLoop, calls=%fused_computation.78 | loop fusion | flops 12224 | bytes 512 | tf_op jit(solution)/shard_map/reduce_sum | solution.py:57
  8.8 0.9 %bitcast_dynamic-update-slice_fusion.7 = bf16[8,4,8192]{2,1,0:T(4,128)(2,1)S(1)} fusion(bf16[4,8192]{1,0:T(4,128)(2,1)} %param.6), kind=kLoop, calls=%fused_computation.42 | loop fusion | bytes 131072
  9.7 0.7 dynamic_slice.72
  10.4 0.1 convert_reduce_fusion
  10.5 0.7 select_reduce_fusion
  11.3 0.7 fusion.31
  12.1 0.6 collective-permute-start.2
  12.7 1.5 %collective-permute-start.6 = (bf16[4,8192]{1,0:T(4,128)(2,1)S(1)}, bf16[4,8192]{1,0:T(4,128)(2,1)S(1)}, u32[]{:S(2)}, u32[]{:S(2)}) collective-permute-start(bf16[4,8192]{1,0:T(4,128)(2,1)S(1)} %collective-permute-done.5), channel_id=1, source_target_pairs={{0,1},{1,0},{2,3},{3,2},{4,5},{5,4},{6,7},{7,6},{8,9},{9,8},{10,11... | collective-permute-start | bytes 196616 | tf_op jit(solution)/shard_map/ppermute | solution.py:15
  14.2 0.6 collective-permute-start.4
  14.9 1.7 %collective-permute-done.2 = bf16[4,8192]{1,0:T(4,128)(2,1)S(1)} collective-permute-done((bf16[4,8192]{1,0:T(4,128)(2,1)S(1)}, bf16[4,8192]{1,0:T(4,128)(2,1)S(1)}, u32[]{:S(2)}, u32[]{:S(2)}) %collective-permute-start.2) | collective-permute-done | bytes 65568 | tf_op jit(solution)/shard_map/ppermute | solution.py:15
  16.7 1.9 %collective-permute-done.4 = bf16[4,8192]{1,0:T(4,128)(2,1)S(1)} collective-permute-done((bf16[4,8192]{1,0:T(4,128)(2,1)S(1)}, bf16[4,8192]{1,0:T(4,128)(2,1)S(1)}, u32[]{:S(2)}, u32[]{:S(2)}) %collective-permute-start.4) | collective-permute-done | bytes 65568 | tf_op jit(solution)/shard_map/ppermute | solution.py:15
  18.7 0.2 dynamic-slice_bitcast_fusion
  18.9 0.3 concatenate.14
  19.3 3.0 %fusion.3 = f32[32,256]{1,0:T(8,128)S(1)} fusion(bf16[32,8192]{1,0:T(8,128)(2,1)S(1)} %concatenate.14, bf16[1,8192,256]{2,1,0:T(8,128)(2,1)} %param.8), kind=kOutput, calls=%fused_computation.3 | convolution fusion | flops 134217728 | bytes 4751360 | tf_op jit(solution)/shard_map/dot_general | solution.py:104
  22.3 8.8 %convolution_bitcast_fusion = f32[4,8,8,128]{3,1,2,0:T(8,128)S(1)} fusion(bf16[32,8192]{1,0:T(8,128)(2,1)S(1)} %concatenate.14, bf16[8192,1024]{1,0:T(8,128)(2,1)} %param.7), kind=kOutput, calls=%fused_computation.7 | convolution fusion | flops 536870912 | bytes 17432576 | tf_op jit(solution)/shard_map/dot_general | solution.py:105
  31.3 0.1 fusion.65
  31.5 1.0 %collective-permute-done.7 = bf16[32,256]{1,0:T(8,128)(2,1)S(1)} collective-permute-done((bf16[32,256]{1,0:T(8,128)(2,1)S(1)}, bf16[32,256]{1,0:T(8,128)(2,1)S(1)}, u32[]{:S(2)}, u32[]{:S(2)}) %collective-permute-start.7) | collective-permute-done | bytes 16416 | tf_op jit(solution)/shard_map/ppermute | solution.py:15
  32.6 0.1 convolution_convert_fusion.1
  32.7 0.6 constant_dynamic-update-slice_fusion.15
  33.3 0.6 constant_dynamic-update-slice_fusion.14
  33.9 0.6 constant_dynamic-update-slice_fusion.13
  34.5 0.6 constant_dynamic-update-slice_fusion.12
  35.0 0.6 constant_dynamic-update-slice_fusion.11
  35.6 0.6 constant_dynamic-update-slice_fusion.10
  36.2 0.6 constant_dynamic-update-slice_fusion.9
  36.8 0.6 constant_dynamic-update-slice_fusion.8
  37.4 0.6 constant_dynamic-update-slice_fusion.7
  37.9 0.6 constant_dynamic-update-slice_fusion.6
  38.5 0.6 constant_dynamic-update-slice_fusion.5
  39.1 0.6 constant_dynamic-update-slice_fusion.4
  39.7 0.6 constant_dynamic-update-slice_fusion.3
  40.3 0.6 constant_dynamic-update-slice_fusion.2
  40.8 0.6 constant_dynamic-update-slice_fusion.1
  41.4 0.4 fusion.66
  41.8 0.6 fusion.9
  42.5 8.6 %fusion.71 = (bf16[8,4,8192]{2,0,1:T(8,128)(2,1)S(1)}, f32[8,4,8192]{2,0,1:T(8,128)S(1)}) fusion(bf16[1024,8192]{1,0:T(8,128)(2,1)} %param.9, bf16[8,4,1024]{2,1,0:T(4,128)(2,1)S(1)} %dot_general.24), kind=kOutput, calls=%fused_computation.145 | convolution fusion | flops 537133056 | bytes 18415616 | tf_op jit(solution)/shard_map/dot_general | solution.py:141
  51.1 1.0 %constant_dynamic-slice_fusion.6 = (bf16[1,4,8192]{2,0,1:T(2,128)(2,1)S(1)}, bf16[1,4,8192]{2,0,1:T(2,128)(2,1)S(1)}, bf16[1,4,8192]{2,0,1:T(2,128)(2,1)S(1)}, b...) fusion(bf16[8,4,8192]{2,0,1:T(8,128)(2,1)S(1)} %get-tuple-eleme, ...), kind=kLoop, calls=%fused_computation.104 | loop fusion | bytes 917532 | tf_op jit(solution)/shard_map/jit(dynamic_index_in_dim)/dynamic_slice | solution.py:49
  52.1 0.1 copy.51
  52.2 0.1 copy.52
  52.3 2.9 %collective-permute-start.9 = (bf16[4,8192]{1,0:T(4,128)(2,1)S(1)}, bf16[4,8192]{1,0:T(4,128)(2,1)S(1)}, u32[]{:S(2)}, u32[]{:S(2)}) collective-permute-start(bf16[4,8192]{1,0:T(4,128)(2,1)S(1)} %bitcast.189), channel_id=1, source_target_pairs={{0,6},{1,7},{2,4},{3,5},{4,2},{5,3},{6,0},{7,1},{8,14},{9,15},{10,... | collective-permute-start | bytes 196616 | tf_op jit(solution)/shard_map/ppermute | solution.py:15
  55.2 0.5 collective-permute-start.10
  55.7 0.6 constant_dynamic-update-slice_fusion
  56.3 4.7 %all-to-all-start = ((bf16[16,1,8,128]{3,2,1,0:T(8,128)(2,1)}), bf16[16,1,8,128]{3,2,1,0:T(8,128)(2,1)S(1)}, u32[]{:S(2)}, u32[]{:S(2)}) async-start(bf16[16,1,8,128]{3,2,1,0:T(8,128)(2,1)} %constant_dynamic-update-slice_fusion), calls=%async_computation | async-start | bytes 65536 | tf_op jit(solution)/shard_map/all_to_all | solution.py:139
  61.0 0.1 copy.53
  61.1 0.1 copy.47
  61.2 0.1 copy.48
  61.3 0.1 copy.49
  61.4 0.1 copy.50
  61.5 2.9 %collective-permute-start.11 = (bf16[4,8192]{1,0:T(4,128)(2,1)S(1)}, bf16[4,8192]{1,0:T(4,128)(2,1)S(1)}, u32[]{:S(2)}, u32[]{:S(2)}) collective-permute-start(bf16[4,8192]{1,0:T(4,128)(2,1)S(1)} %bitcast.190), channel_id=1, source_target_pairs={{0,4},{1,5},{2,6},{3,7},{4,0},{5,1},{6,2},{7,3},{8,12},{9,13},{10,... | collective-permute-start | bytes 196616 | tf_op jit(solution)/shard_map/ppermute | solution.py:15
  64.4 2.4 %collective-permute-start.12 = (bf16[4,8192]{1,0:T(4,128)(2,1)S(1)}, bf16[4,8192]{1,0:T(4,128)(2,1)S(1)}, u32[]{:S(2)}, u32[]{:S(2)}) collective-permute-start(bf16[4,8192]{1,0:T(4,128)(2,1)S(1)} %bitcast.188), channel_id=1, source_target_pairs={{0,3},{1,2},{2,1},{3,0},{4,7},{5,6},{6,5},{7,4},{8,11},{9,10},{10,... | collective-permute-start | bytes 196616 | tf_op jit(solution)/shard_map/ppermute | solution.py:15
  66.8 0.6 collective-permute-start.13
  67.3 0.6 collective-permute-start.14
  67.9 2.4 %collective-permute-start.8 = (bf16[4,8192]{1,0:T(4,128)(2,1)S(1)}, bf16[4,8192]{1,0:T(4,128)(2,1)S(1)}, u32[]{:S(2)}, u32[]{:S(2)}) collective-permute-start(bf16[4,8192]{1,0:T(4,128)(2,1)S(1)} %bitcast.184), channel_id=1, source_target_pairs={{0,7},{1,6},{2,5},{3,4},{4,3},{5,2},{6,1},{7,0},{8,15},{9,14},{10,... | collective-permute-start | bytes 196616 | tf_op jit(solution)/shard_map/ppermute | solution.py:15
  70.3 0.1 constant_dynamic-slice_fusion.7
  70.4 0.4 collective-permute-done.12
  70.8 0.4 collective-permute-done.13
  71.2 0.4 collective-permute-done.14
  71.6 3.3 %collective-permute-done.8 = bf16[4,8192]{1,0:T(4,128)(2,1)S(1)} collective-permute-done((bf16[4,8192]{1,0:T(4,128)(2,1)S(1)}, bf16[4,8192]{1,0:T(4,128)(2,1)S(1)}, u32[]{:S(2)}, u32[]{:S(2)}) %collective-permute-start.8) | collective-permute-done | bytes 65568 | tf_op jit(solution)/shard_map/ppermute | solution.py:15
  74.9 0.8 %fusion.16 = bf16[4,8192]{1,0:T(4,128)(2,1)} fusion(bf16[4,8192]{1,0:T(4,128)(2,1)S(1)} %collective-permute-done.14, bf16[4,8192]{1,0:T(4,128)(2,1)S(1)} %collective-permute-done.13, bf16[4,8192]{1,0:T(4,128)(2,1)S(1)} %collective-permute-done.12, bf16[4,8192]{1,0:T(4,128)(2,1)S(1)} %collective-permute-done.11, ...), kind=kLoop, calls=%fused_computation.24 | loop fusion | flops 491520 | bytes 655360 | tf_op jit(solution)/shard_map/convert_element_type | solution.py:142
  75.7 0.6 copy.77
  (33 shorter events, 0.9 us)
Async XLA Ops:
  0.6 11.5 %collective-permute-start.1 = (bf16[4,8192]{1,0:T(4,128)(2,1)}, bf16[4,8192]{1,0:T(4,128)(2,1)S(1)}, u32[]{:S(2)}, u32[]{:S(2)}) collective-permute-start(bf16[4,8192]{1,0:T(4,128)(2,1)} %param.6), channel_id=1, source_target_pairs={{0,2},{1,3},{2,0},{3,1},{4,6},{5,7},{6,4},{7,5},{8,10},{9,11},{10,... | collective-permute-start | bytes 196616 | tf_op jit(solution)/shard_map/ppermute | solution.py:15
  3.7 11.1 %collective-permute-start = (bf16[4,8192]{1,0:T(4,128)(2,1)}, bf16[4,8192]{1,0:T(4,128)(2,1)S(1)}, u32[]{:S(2)}, u32[]{:S(2)}) collective-permute-start(bf16[4,8192]{1,0:T(4,128)(2,1)} %param.6), channel_id=1, source_target_pairs={{0,1},{1,0},{2,3},{3,2},{4,5},{5,4},{6,7},{7,6},{8,9},{9,8},{10,11... | collective-permute-start | bytes 196616 | tf_op jit(solution)/shard_map/ppermute | solution.py:15
  5.2 7.5 %collective-permute-start.5 = (bf16[4,8192]{1,0:T(4,128)(2,1)}, bf16[4,8192]{1,0:T(4,128)(2,1)S(1)}, u32[]{:S(2)}, u32[]{:S(2)}) collective-permute-start(bf16[4,8192]{1,0:T(4,128)(2,1)} %param.6), channel_id=1, source_target_pairs={{0,6},{1,7},{2,4},{3,5},{4,2},{5,3},{6,0},{7,1},{8,14},{9,15},{10,... | collective-permute-start | bytes 196616 | tf_op jit(solution)/shard_map/ppermute | solution.py:15
  7.7 6.5 %collective-permute-start.3 = (bf16[4,8192]{1,0:T(4,128)(2,1)}, bf16[4,8192]{1,0:T(4,128)(2,1)S(1)}, u32[]{:S(2)}, u32[]{:S(2)}) collective-permute-start(bf16[4,8192]{1,0:T(4,128)(2,1)} %param.6), channel_id=1, source_target_pairs={{0,4},{1,5},{2,6},{3,7},{4,0},{5,1},{6,2},{7,3},{8,12},{9,13},{10,... | collective-permute-start | bytes 196616 | tf_op jit(solution)/shard_map/ppermute | solution.py:15
  12.1 4.5 %collective-permute-start.2 = (bf16[4,8192]{1,0:T(4,128)(2,1)S(1)}, bf16[4,8192]{1,0:T(4,128)(2,1)S(1)}, u32[]{:S(2)}, u32[]{:S(2)}) collective-permute-start(bf16[4,8192]{1,0:T(4,128)(2,1)S(1)} %collective-permute-done.1), channel_id=1, source_target_pairs={{0,1},{1,0},{2,3},{3,2},{4,5},{5,4},{6,7},{7,6},{8,9},{9,8},{10,11... | collective-permute-start | bytes 196616 | tf_op jit(solution)/shard_map/ppermute | solution.py:15
  12.7 5.9 %collective-permute-start.6 = (bf16[4,8192]{1,0:T(4,128)(2,1)S(1)}, bf16[4,8192]{1,0:T(4,128)(2,1)S(1)}, u32[]{:S(2)}, u32[]{:S(2)}) collective-permute-start(bf16[4,8192]{1,0:T(4,128)(2,1)S(1)} %collective-permute-done.5), channel_id=1, source_target_pairs={{0,1},{1,0},{2,3},{3,2},{4,5},{5,4},{6,7},{7,6},{8,9},{9,8},{10,11... | collective-permute-start | bytes 196616 | tf_op jit(solution)/shard_map/ppermute | solution.py:15
  14.2 4.3 %collective-permute-start.4 = (bf16[4,8192]{1,0:T(4,128)(2,1)S(1)}, bf16[4,8192]{1,0:T(4,128)(2,1)S(1)}, u32[]{:S(2)}, u32[]{:S(2)}) collective-permute-start(bf16[4,8192]{1,0:T(4,128)(2,1)S(1)} %collective-permute-done.3), channel_id=1, source_target_pairs={{0,1},{1,0},{2,3},{3,2},{4,5},{5,4},{6,7},{7,6},{8,9},{9,8},{10,11... | collective-permute-start | bytes 196616 | tf_op jit(solution)/shard_map/ppermute | solution.py:15
  31.3 1.2 %collective-permute-start.7 = (bf16[32,256]{1,0:T(8,128)(2,1)S(1)}, bf16[32,256]{1,0:T(8,128)(2,1)S(1)}, u32[]{:S(2)}, u32[]{:S(2)}) collective-permute-start(bf16[32,256]{1,0:T(8,128)(2,1)S(1)} %pad_maximum_fusion), channel_id=1, source_target_pairs={{0,8},{8,0},{1,9},{9,1},{2,10},{10,2},{3,11},{11,3},{4,12},{12,4},... | collective-permute-start | bytes 49160 | tf_op jit(solution)/shard_map/ppermute | solution.py:15
  52.3 15.0 %collective-permute-start.9 = (bf16[4,8192]{1,0:T(4,128)(2,1)S(1)}, bf16[4,8192]{1,0:T(4,128)(2,1)S(1)}, u32[]{:S(2)}, u32[]{:S(2)}) collective-permute-start(bf16[4,8192]{1,0:T(4,128)(2,1)S(1)} %bitcast.189), channel_id=1, source_target_pairs={{0,6},{1,7},{2,4},{3,5},{4,2},{5,3},{6,0},{7,1},{8,14},{9,15},{10,... | collective-permute-start | bytes 196616 | tf_op jit(solution)/shard_map/ppermute | solution.py:15
  55.2 12.7 %collective-permute-start.10 = (bf16[4,8192]{1,0:T(4,128)(2,1)S(1)}, bf16[4,8192]{1,0:T(4,128)(2,1)S(1)}, u32[]{:S(2)}, u32[]{:S(2)}) collective-permute-start(bf16[4,8192]{1,0:T(4,128)(2,1)S(1)} %bitcast.187), channel_id=1, source_target_pairs={{0,5},{1,4},{2,7},{3,6},{4,1},{5,0},{6,3},{7,2},{8,13},{9,12},{10,... | collective-permute-start | bytes 196616 | tf_op jit(solution)/shard_map/ppermute | solution.py:15
  56.3 14.1 %all-to-all-start = ((bf16[16,1,8,128]{3,2,1,0:T(8,128)(2,1)}), bf16[16,1,8,128]{3,2,1,0:T(8,128)(2,1)S(1)}, u32[]{:S(2)}, u32[]{:S(2)}) async-start(bf16[16,1,8,128]{3,2,1,0:T(8,128)(2,1)} %constant_dynamic-update-slice_fusion), calls=%async_computation | async-start | bytes 65536 | tf_op jit(solution)/shard_map/all_to_all | solution.py:139
  61.5 8.9 %collective-permute-start.11 = (bf16[4,8192]{1,0:T(4,128)(2,1)S(1)}, bf16[4,8192]{1,0:T(4,128)(2,1)S(1)}, u32[]{:S(2)}, u32[]{:S(2)}) collective-permute-start(bf16[4,8192]{1,0:T(4,128)(2,1)S(1)} %bitcast.190), channel_id=1, source_target_pairs={{0,4},{1,5},{2,6},{3,7},{4,0},{5,1},{6,2},{7,3},{8,12},{9,13},{10,... | collective-permute-start | bytes 196616 | tf_op jit(solution)/shard_map/ppermute | solution.py:15
  64.4 6.4 %collective-permute-start.12 = (bf16[4,8192]{1,0:T(4,128)(2,1)S(1)}, bf16[4,8192]{1,0:T(4,128)(2,1)S(1)}, u32[]{:S(2)}, u32[]{:S(2)}) collective-permute-start(bf16[4,8192]{1,0:T(4,128)(2,1)S(1)} %bitcast.188), channel_id=1, source_target_pairs={{0,3},{1,2},{2,1},{3,0},{4,7},{5,6},{6,5},{7,4},{8,11},{9,10},{10,... | collective-permute-start | bytes 196616 | tf_op jit(solution)/shard_map/ppermute | solution.py:15
  66.8 4.4 %collective-permute-start.13 = (bf16[4,8192]{1,0:T(4,128)(2,1)S(1)}, bf16[4,8192]{1,0:T(4,128)(2,1)S(1)}, u32[]{:S(2)}, u32[]{:S(2)}) collective-permute-start(bf16[4,8192]{1,0:T(4,128)(2,1)S(1)} %bitcast.186), channel_id=1, source_target_pairs={{0,2},{1,3},{2,0},{3,1},{4,6},{5,7},{6,4},{7,5},{8,10},{9,11},{10,... | collective-permute-start | bytes 196616 | tf_op jit(solution)/shard_map/ppermute | solution.py:15
  67.3 4.3 %collective-permute-start.14 = (bf16[4,8192]{1,0:T(4,128)(2,1)S(1)}, bf16[4,8192]{1,0:T(4,128)(2,1)S(1)}, u32[]{:S(2)}, u32[]{:S(2)}) collective-permute-start(bf16[4,8192]{1,0:T(4,128)(2,1)S(1)} %bitcast.185), channel_id=1, source_target_pairs={{0,1},{1,0},{2,3},{3,2},{4,5},{5,4},{6,7},{7,6},{8,9},{9,8},{10,11... | collective-permute-start | bytes 196616 | tf_op jit(solution)/shard_map/ppermute | solution.py:15
  67.9 7.0 %collective-permute-start.8 = (bf16[4,8192]{1,0:T(4,128)(2,1)S(1)}, bf16[4,8192]{1,0:T(4,128)(2,1)S(1)}, u32[]{:S(2)}, u32[]{:S(2)}) collective-permute-start(bf16[4,8192]{1,0:T(4,128)(2,1)S(1)} %bitcast.184), channel_id=1, source_target_pairs={{0,7},{1,6},{2,5},{3,4},{4,3},{5,2},{6,1},{7,0},{8,15},{9,14},{10,... | collective-permute-start | bytes 196616 | tf_op jit(solution)/shard_map/ppermute | solution.py:15
